TPU v7x, 32 devices: a whole 2x2x4 slice. The times are simulated.
32 devices in a mesh: row: 8 (over z, x), col: 4 (over y, core).
Axes of the slice: x: 2, y: 2, z: 4, core: 2. Of those that a mesh axis runs over, the one named last changes fastest.
Arguments:
- density_first: bfloat16 [12288, 12288], P('row', 'col'), may hold values from -0.0068359375 to 0.0068359375
- density_second: bfloat16 [12288, 12288], P('row', 'col'), may hold values from -0.0068359375 to 0.0068359375
- basis: bfloat16 [64, 4096, 896], P(('row', 'col')), may hold values from -6 to 6
- tile_list: int32 [64, 7], P(('row', 'col')), may hold values from 0 to 95, as said below
- tile_count: int32 [64], P(('row', 'col')), may hold values from 5 to 7, as said below
- point_count: int32 [64], P(('row', 'col')), may hold values from 1024 to 4096, as said below
- offsets: float32 [3, 64, 4096], P(None, ('row', 'col')), may hold values from -5 to 5
- weights: float32 [64, 4096], P(('row', 'col')), may hold values from 0.05 to 1
- atom_of_point: int32 [64, 4096], P(('row', 'col')), may hold values from 0 to 1023, as said below
Outputs:
- density: float32 [2, 64, 4096], P(None, ('row', 'col'))
- moments: float32 [2, 9, 1024], replicated
Inputs may be any that keep to these rules, and one draw needn't show every extreme that they name: `tile_list`: the 7 tile numbers of each batch are 7 consecutive numbers in some order. `tile_count`: some batch has 7. `point_count`: some batch has 4096. `atom_of_point`: the points of batch g belong to atoms (g * 16 + j) mod 1024 with j from 0 to 7.
All inputs are finite; a program needn't handle non-finite values.
Results may differ from a plain program's by a relative error of at most 0.0003.
Values may be sent and summed in bfloat16 or wider, within the bound.
A program may use at most 192 MiB of HBM per device.

v0:
```python
import jax
import jax.numpy as jnp
from jax import lax
from jax.sharding import PartitionSpec as P

TILE = 128
ATOMS = 1024


def harmonics(offsets):
    first_axis = offsets[0]
    second_axis = offsets[1]
    third_axis = offsets[2]
    radius_sq = first_axis * first_axis + second_axis * second_axis + third_axis * third_axis
    return jnp.stack(
        [
            jnp.ones_like(first_axis),
            first_axis,
            second_axis,
            third_axis,
            first_axis * second_axis,
            second_axis * third_axis,
            3.0 * third_axis * third_axis - radius_sq,
            first_axis * third_axis,
            first_axis * first_axis - second_axis * second_axis,
        ]
    )


def local(
    density_first,
    density_second,
    basis,
    tile_list,
    tile_count,
    point_count,
    offsets,
    weights,
    atom_of_point,
):
    row_count = lax.axis_size("row")
    col_count = lax.axis_size("col")
    tile_size = TILE
    local_rows = density_first.shape[0] // tile_size
    local_cols = density_first.shape[1] // tile_size
    batches_dev = tile_list.shape[0]
    run_length = tile_list.shape[1]
    points = basis.shape[1]
    row_slots = -(-run_length // row_count)
    col_slots = -(-run_length // col_count)
    my_row = lax.axis_index("row")
    my_col = lax.axis_index("col")
    own_start = jnp.min(tile_list, axis=1)
    starts = lax.all_gather(own_start, ("row", "col"), axis=0, tiled=True)
    run_end = starts[:, None] + run_length
    first_row = starts + (my_row - starts) % row_count
    row_tile = first_row[:, None] + row_count * jnp.arange(row_slots, dtype=jnp.int32)[None, :]
    row_ok = row_tile < run_end
    row_local = jnp.where(row_ok, row_tile // row_count, 0)
    first_col = starts + (my_col - starts) % col_count
    col_tile = first_col[:, None] + col_count * jnp.arange(col_slots, dtype=jnp.int32)[None, :]
    col_ok = col_tile < run_end
    col_local = jnp.where(col_ok, col_tile // col_count, 0)
    wanted = row_ok[:, :, None] & col_ok[:, None, :]

    def pack_tiles(stored):
        tile_grid = stored.reshape(local_rows, tile_size, local_cols, tile_size).transpose(
            0, 2, 1, 3
        )
        picked = tile_grid[row_local[:, :, None], col_local[:, None, :]]
        picked = jnp.where(wanted[..., None, None], picked, jnp.zeros((), stored.dtype))
        return picked.reshape(
            row_count, col_count, batches_dev, row_slots, col_slots, tile_size, tile_size
        )

    outgoing_first = pack_tiles(density_first)
    outgoing_second = pack_tiles(density_second)
    flat_shape = (row_count * col_count,) + outgoing_first.shape[2:]
    flat_first = outgoing_first.reshape(flat_shape)
    flat_second = outgoing_second.reshape(flat_shape)
    moved_first, moved_second = (
        lax.all_to_all(flat_first, ("row", "col"), split_axis=0, concat_axis=0, tiled=True),
        lax.all_to_all(flat_second, ("row", "col"), split_axis=0, concat_axis=0, tiled=True),
    )
    arrived_first = moved_first.reshape(outgoing_first.shape)
    arrived_second = moved_second.reshape(outgoing_second.shape)
    offset_in_run = tile_list - own_start[:, None]
    owner_row = tile_list % row_count
    slot_row = offset_in_run // row_count
    owner_col = tile_list % col_count
    slot_col = offset_in_run // col_count
    batch_ids = jnp.arange(batches_dev, dtype=jnp.int32)[:, None, None]

    def assemble(arrived):
        blocks = arrived[
            owner_row[:, :, None],
            owner_col[:, None, :],
            batch_ids,
            slot_row[:, :, None],
            slot_col[:, None, :],
        ]
        return blocks.transpose(0, 1, 3, 2, 4).reshape(
            batches_dev, run_length * tile_size, run_length * tile_size
        )

    col_mask = jnp.arange(run_length)[None, :] < tile_count[:, None]
    col_mask = jnp.repeat(col_mask, tile_size, axis=1).astype(jnp.bfloat16)
    masked = basis * col_mask[:, None, :]
    point_mask = (jnp.arange(points)[None, :] < point_count[:, None]).astype(jnp.float32)

    def density_of(arrived):
        block = assemble(arrived)
        product = jnp.einsum("bpi,bij->bpj", masked, block, preferred_element_type=jnp.float32)
        return jnp.sum(product * masked.astype(jnp.float32), axis=2) * point_mask

    density = jnp.stack([density_of(arrived_first), density_of(arrived_second)])
    harmonic = harmonics(offsets)
    moment_terms = density[:, None] * (weights[None, None] * harmonic[None])
    flat_terms = moment_terms.reshape(2 * 9, -1)
    one_hot = (
        atom_of_point.reshape(-1)[:, None] == jnp.arange(ATOMS, dtype=jnp.int32)[None, :]
    ).astype(jnp.float32)
    partial_value = jnp.dot(
        flat_terms, one_hot, precision=lax.Precision.HIGHEST, preferred_element_type=jnp.float32
    )
    moments = lax.psum(partial_value, ("row", "col"))
    return (density, moments.reshape(2, 9, ATOMS))


def solution(mesh):
    placed = (
        P("row", "col"),
        P("row", "col"),
        P(("row", "col"), None, None),
        P(("row", "col"), None),
        P(("row", "col")),
        P(("row", "col")),
        P(None, ("row", "col"), None),
        P(("row", "col"), None),
        P(("row", "col"), None),
    )
    return jax.shard_map(
        local,
        mesh=mesh,
        in_specs=placed,
        out_specs=(P(None, ("row", "col"), None), P()),
        check_vma=False,
    )
```

profile of v0, /device:TPU:0, one launch (start us, length us, event | category | flops | bytes accessed | tf_op | source)
XLA Modules:
  0.0 516.1 jit_solution(7729851914212681637)
XLA Ops:
  7.2 0.8 fusion.11
  8.0 0.2 dynamic-update-slice
  8.2 42.0 %all-reduce = s32[64]{0:T(128)S(1)} all-reduce(s32[64]{0:T(128)S(1)} %dynamic-update-slice), channel_id=1, replica_groups=mesh['row'=8,'col'=4] {'row','col'}, use_global_device_ids=true, to_apply=%add | all-reduce | flops 64 | bytes 512
  50.7 0.1 reshape.452
  50.8 9.8 %copy.68 = bf16[192,8,24,128]{3,2,1,0:T(8,128)(2,1)} copy(bf16[192,8,24,128]{3,1,2,0:T(8,128)(2,1)} %bitcast.60) | data formatting | bytes 18874368
  60.6 10.0 %copy.75 = bf16[12,128,24,128]{3,1,2,0:T(8,128)(2,1)} copy(bf16[12,128,24,128]{3,2,1,0:T(8,128)(2,1)} %bitcast.51) | data formatting | bytes 18874368 | tf_op jit(solution)/shard_map/reshape | solution.py:67
  70.6 9.9 %copy.67 = bf16[192,8,24,128]{3,2,1,0:T(8,128)(2,1)} copy(bf16[192,8,24,128]{3,1,2,0:T(8,128)(2,1)} %bitcast.61) | data formatting | bytes 18874368
  80.5 10.1 %copy.76 = bf16[12,128,24,128]{3,1,2,0:T(8,128)(2,1)} copy(bf16[12,128,24,128]{3,2,1,0:T(8,128)(2,1)} %bitcast.52) | data formatting | bytes 18874368 | tf_op jit(solution)/shard_map/reshape | solution.py:67
  90.6 6.8 %gather_fusion.2 = bf16[128,128,128]{2,1,0:T(8,128)(2,1)} fusion(bf16[12,24,128,128]{3,2,1,0:T(8,128)(2,1)} %bitcast.53, s32[128]{0:T(128)S(1)} %reshape.452), kind=kCustom, calls=%fused_computation.2 | custom fusion | bytes 8389632 | tf_op jit(solution)/shard_map/gather | solution.py:70
  97.4 6.7 %gather_fusion = bf16[128,128,128]{2,1,0:T(8,128)(2,1)} fusion(bf16[12,24,128,128]{3,2,1,0:T(8,128)(2,1)} %bitcast.54, s32[128]{0:T(128)S(1)} %reshape.452), kind=kCustom, calls=%fused_computation | custom fusion | bytes 8389632 | tf_op jit(solution)/shard_map/gather | solution.py:70
  104.3 0.2 compare_and_fusion
  104.5 5.2 broadcast_select_fusion.1
  109.6 97.9 %all_to_all.10 = bf16[32,2,1,2,128,128]{5,4,3,1,2,0:T(8,128)(2,1)} all-to-all(bf16[32,2,1,2,128,128]{5,4,3,1,2,0:T(8,128)(2,1)S(1)} %get-tuple-element.13), channel_id=1, replica_groups=mesh['row'=8,'col'=4] {'row','col'}, dimensions={0} | all-to-all | bytes 8388608 | tf_op jit(solution)/shard_map/all_to_all | solution.py:83
  207.5 3.8 all-to-all-start
  211.3 0.5 all-reduce.3.cloned.1.call-start
  212.2 19.9 %copy.46 = bf16[2,4096,896]{1,2,0:T(8,128)(2,1)} copy(bf16[2,4096,896]{2,1,0:T(8,128)(2,1)} %param.11) | data formatting | bytes 29360128 | tf_op args[2]
  232.6 4.2 gather_fusion.3
  236.9 4.5 copy.56
  241.4 7.4 %reshape.487 = bf16[2,896,896]{2,1,0:T(8,128)(2,1)} reshape(bf16[2,7,128,7,128]{4,3,2,1,0:T(8,128)(2,1)} %copy.56) | data formatting | bytes 6422528 | tf_op jit(solution)/shard_map/reshape | solution.py:102
  248.8 56.7 %all-to-all-done = bf16[32,2,1,2,128,128]{5,4,3,1,2,0:T(8,128)(2,1)} async-done(((bf16[32,2,1,2,128,128]{5,4,3,1,2,0:T(8,128)(2,1)}), bf16[32,2,1,2,128,128]{5,4,3,1,2,0:T(8,128)(2,1)}, u32[]{:S(2)}, u32[]{:S(2)}) %all-to-all-start) | async-done | bytes 4194336 | tf_op jit(solution)/shard_map/all_to_all | solution.py:82
  305.6 4.2 gather_fusion.1
  309.8 4.5 copy.51
  314.3 7.6 %reshape.485 = bf16[2,896,896]{2,1,0:T(8,128)(2,1)} reshape(bf16[2,7,128,7,128]{4,3,2,1,0:T(8,128)(2,1)} %copy.51) | data formatting | bytes 6422528 | tf_op jit(solution)/shard_map/reshape | solution.py:102
  321.9 23.4 %fusion.2 = f32[2,4096]{1,0:T(2,128)S(1)} fusion(bf16[2,896,896]{2,1,0:T(8,128)(2,1)S(1)} %copy-done, bf16[2,4096,896]{1,2,0:T(8,128)(2,1)} %copy.46, bf16[2,896]{1,0:T(2,128)(2,1)S(1)} %bitcast.68), kind=kOutput, calls=%fused_computation.9 | convolution fusion | flops 13190029312 | bytes 17927680 | tf_op jit(solution)/shard_map/bpi,bij->bpj/dot_general | solution.py:113
  345.3 24.4 %fusion.1 = f32[2,4096]{1,0:T(2,128)S(1)} fusion(bf16[2,896,896]{2,1,0:T(8,128)(2,1)} %reshape.485, bf16[2,4096,896]{1,2,0:T(8,128)(2,1)} %copy.46, bf16[2,896]{1,0:T(2,128)(2,1)S(1)} %bitcast.69), kind=kOutput, calls=%fused_computation.8 | convolution fusion | flops 13190029312 | bytes 17927680 | tf_op jit(solution)/shard_map/bpi,bij->bpj/dot_general | solution.py:113
  369.9 0.2 broadcast_multiply_fusion
  370.2 0.4 pad.4
  370.5 0.5 copy.69
  371.0 10.5 %fusion = f32[18,1024]{1,0:T(8,128)S(1)} fusion(f32[18,8192]{1,0:T(8,128)S(1)} %bitcast.64, s32[8192]{0:T(1024)S(1)} %bitcast.66), kind=kOutput, calls=%fused_computation.7 | convolution fusion | flops 1820327936 | bytes 696320 | tf_op jit(solution)/shard_map/dot_general | solution.py:123
  381.5 0.7 reshape.449
  382.2 125.1 %all-reduce.3.cloned.1.call-done = f32[2,9,1024]{2,1,0:T(8,128)} async-done(((f32[2,9,1024]{2,1,0:T(8,128)}), f32[2,9,1024]{2,1,0:T(8,128)}) %all-reduce.3.cloned.1.call-update) | async-done | bytes 73744 | tf_op jit(solution)/shard_map/psum | solution.py:126
  507.3 1.6 copy.59
  (47 shorter events, 1.4 us)
Async XLA Ops:
  207.5 4.3 copy-start.5
  207.5 98.0 %all-to-all-start = ((bf16[32,2,1,2,128,128]{5,4,3,1,2,0:T(8,128)(2,1)}), bf16[32,2,1,2,128,128]{5,4,3,1,2,0:T(8,128)(2,1)}, u32[]{:S(2)}, u32[]{:S(2)}) async-start(bf16[32,2,1,2,128,128]{5,4,3,1,2,0:T(8,128)(2,1)} %get-tuple-element.12), calls=%async_computation | async-start | bytes 8388608 | tf_op jit(solution)/shard_map/all_to_all | solution.py:82
  211.3 295.9 %all-reduce.3.cloned.1.call-start = ((), (), s32[]{:S(2)}) async-start(), calls=%async_computation.2 | async-start | bytes 262144 | tf_op jit(solution)/shard_map/psum | solution.py:126
  212.1 20.0 %copy-start.7 = (s32[2]{0:T(128)S(1)}, s32[2]{0:T(128)}, u32[]{:S(2)}) copy-start(s32[2]{0:T(128)} %param.13) | copy-start | bytes 28
  212.1 20.1 %copy-start.4 = (s32[2,4096]{1,0:T(2,128)S(1)}, s32[2,4096]{1,0:T(2,128)}, u32[]{:S(2)}) copy-start(s32[2,4096]{1,0:T(2,128)} %param.17) | copy-start | bytes 98308
  212.1 20.1 %copy-start.1 = (f32[3,2,4096]{2,1,0:T(2,128)S(1)}, f32[3,2,4096]{2,1,0:T(2,128)}, u32[]{:S(2)}) copy-start(f32[3,2,4096]{2,1,0:T(2,128)} %param.15) | copy-start | bytes 294916
  212.2 20.3 %copy-start.3 = (f32[2,4096]{1,0:T(2,128)S(1)}, f32[2,4096]{1,0:T(2,128)}, u32[]{:S(2)}) copy-start(f32[2,4096]{1,0:T(2,128)} %param.16) | copy-start | bytes 98308
  314.3 7.6 %copy-start = (bf16[2,896,896]{2,1,0:T(8,128)(2,1)S(1)}, bf16[2,896,896]{2,1,0:T(8,128)(2,1)}, u32[]{:S(2)}) copy-start(bf16[2,896,896]{2,1,0:T(8,128)(2,1)} %reshape.487) | copy-start | bytes 9633796
  345.3 24.5 %copy-start.6 = (s32[2]{0:T(128)S(1)}, s32[2]{0:T(128)}, u32[]{:S(2)}) copy-start(s32[2]{0:T(128)} %param.14) | copy-start | bytes 28
  369.9 11.6 %copy-start.2 = (f32[2,2,4096]{2,1,0:T(2,128)}, f32[2,2,4096]{2,1,0:T(2,128)S(1)}, u32[]{:S(2)}) copy-start(f32[2,2,4096]{2,1,0:T(2,128)S(1)} %pad_maximum_fusion) | copy-start | bytes 196612
Sparse Core Ops, SparseCore 0:
  382.3 124.9 all-reduce.2
where the time goes:
time: 525 us; the launch traced here: 516 us
  waiting for transfers between devices  182 us (35%)
  blocking collectives  140 us (27%)
  local copies, waits for them, and re-layouts  110 us (21%)
  matrix products  58.4 us (11%)
  between operations  14.7 us (3%)
  other arithmetic  7.15 us (1%)
    psum x1, waiting for transfers between devices, local(): moments = lax.psum(partial_value, ('row', 'col'))  125 us
    all_to_all x1, blocking collectives, local(): lax.all_to_all(flat_second, ('row', 'col'), split_axis=0, concat_axis=0,...  97.9 us
    all_to_all x1, waiting for transfers between devices, local(): lax.all_to_all(flat_first, ('row', 'col'), split_axis=0, concat_axis=0, t...  56.7 us
    dot_general x2, matrix products, density_of(): jnp.einsum('bpi,bij->bpj', masked, block, preferred_element_type=jnp.floa...  47.8 us
    unnamed x29, local copies, waits for them, and re-layouts  42.4 us
    unnamed x1, blocking collectives  42 us
    reshape x2, local copies, waits for them, and re-layouts, pack_tiles(): stored.reshape(local_rows, tile_size, local_cols, tile_size)  20.1 us
    reshape x2, local copies, waits for them, and re-layouts, assemble(): blocks.transpose(0, 1, 3, 2, 4)  15 us
  transfers between devices with their start and end apart: 2, of which 2 were waited for; matrix products, arithmetic and copies ran while one was open for 7% of the time, Pallas kernels for 0%

commit v1 on v0

--- a/solution.py
+++ b/solution.py
@@ -123,7 +123,7 @@
     partial_value = jnp.dot(
         flat_terms, one_hot, precision=lax.Precision.HIGHEST, preferred_element_type=jnp.float32
     )
-    moments = lax.psum(partial_value, ("row", "col"))
+    moments = lax.psum(lax.psum(partial_value, "col"), "row")
     return (density, moments.reshape(2, 9, ATOMS))
 
 

time: 525 us -> 506 us (0.964)
  waiting for transfers between devices: 182 us -> 161 us
    psum x1 -> x2, waiting for transfers between devices: 125 us -> 105 us  [local(): moments = lax.psum(lax.psum(partial_value, 'col'), 'row')]
  transfers between devices with their start and end apart: 2 -> 3, of which waited for: 2 -> 3; matrix products, arithmetic and copies ran while one was open for 7% -> 7% of each run, Pallas kernels for 0% -> 0%
where the time goes in v1:
time: 506 us; the launch traced here: 497 us
  waiting for transfers between devices  161 us (32%)
  blocking collectives  140 us (28%)
  local copies, waits for them, and re-layouts  111 us (22%)
  matrix products  59 us (12%)
  between operations  14.7 us (3%)
  other arithmetic  7.15 us (1%)
    psum x2, waiting for transfers between devices, local(): moments = lax.psum(lax.psum(partial_value, 'col'), 'row')  105 us
    all_to_all x1, blocking collectives, local(): lax.all_to_all(flat_second, ('row', 'col'), split_axis=0, concat_axis=0,...  97.9 us
    all_to_all x1, waiting for transfers between devices, local(): lax.all_to_all(flat_first, ('row', 'col'), split_axis=0, concat_axis=0, t...  56.7 us
    dot_general x2, matrix products, density_of(): jnp.einsum('bpi,bij->bpj', masked, block, preferred_element_type=jnp.floa...  47.8 us
    unnamed x29, local copies, waits for them, and re-layouts  42.4 us
    unnamed x1, blocking collectives  42 us
    reshape x2, local copies, waits for them, and re-layouts, pack_tiles(): stored.reshape(local_rows, tile_size, local_cols, tile_size)  20.1 us
    reshape x2, local copies, waits for them, and re-layouts, assemble(): blocks.transpose(0, 1, 3, 2, 4)  15 us
  transfers between devices with their start and end apart: 3, of which 3 were waited for; matrix products, arithmetic and copies ran while one was open for 7% of the time, Pallas kernels for 0%

profile of v1, /device:TPU:0, one launch (start us, length us, event | category | flops | bytes accessed | tf_op | source)
XLA Modules:
  0.0 497.2 jit_solution(14238402267019507991)
XLA Ops:
  7.2 0.8 fusion.11
  8.0 0.2 dynamic-update-slice
  8.2 42.0 %all-reduce = s32[64]{0:T(128)S(1)} all-reduce(s32[64]{0:T(128)S(1)} %dynamic-update-slice), channel_id=1, replica_groups=mesh['row'=8,'col'=4] {'row','col'}, use_global_device_ids=true, to_apply=%add | all-reduce | flops 64 | bytes 512
  50.8 9.8 %copy.68 = bf16[192,8,24,128]{3,2,1,0:T(8,128)(2,1)} copy(bf16[192,8,24,128]{3,1,2,0:T(8,128)(2,1)} %bitcast.60) | data formatting | bytes 18874368
  60.6 10.0 %copy.75 = bf16[12,128,24,128]{3,1,2,0:T(8,128)(2,1)} copy(bf16[12,128,24,128]{3,2,1,0:T(8,128)(2,1)} %bitcast.51) | data formatting | bytes 18874368 | tf_op jit(solution)/shard_map/reshape | solution.py:67
  70.6 9.9 %copy.67 = bf16[192,8,24,128]{3,2,1,0:T(8,128)(2,1)} copy(bf16[192,8,24,128]{3,1,2,0:T(8,128)(2,1)} %bitcast.61) | data formatting | bytes 18874368
  80.5 10.1 %copy.76 = bf16[12,128,24,128]{3,1,2,0:T(8,128)(2,1)} copy(bf16[12,128,24,128]{3,2,1,0:T(8,128)(2,1)} %bitcast.52) | data formatting | bytes 18874368 | tf_op jit(solution)/shard_map/reshape | solution.py:67
  90.6 6.8 %gather_fusion.2 = bf16[128,128,128]{2,1,0:T(8,128)(2,1)} fusion(bf16[12,24,128,128]{3,2,1,0:T(8,128)(2,1)} %bitcast.53, s32[128]{0:T(128)S(1)} %reshape.452), kind=kCustom, calls=%fused_computation.2 | custom fusion | bytes 8389632 | tf_op jit(solution)/shard_map/gather | solution.py:70
  97.4 6.7 %gather_fusion = bf16[128,128,128]{2,1,0:T(8,128)(2,1)} fusion(bf16[12,24,128,128]{3,2,1,0:T(8,128)(2,1)} %bitcast.54, s32[128]{0:T(128)S(1)} %reshape.452), kind=kCustom, calls=%fused_computation | custom fusion | bytes 8389632 | tf_op jit(solution)/shard_map/gather | solution.py:70
  104.3 0.2 compare_and_fusion
  104.5 5.2 %broadcast_select_fusion.1 = (bf16[32,2,1,2,128,128]{5,4,3,1,2,0:T(8,128)(2,1)}, bf16[32,2,1,2,128,128]{5,4,3,1,2,0:T(8,128)(2,1)S(1)}) fusion(bf16[32,2,1,2,128,128]{5,4,3,1,2,0:T(8,128)(2,1)} %bitcast.56, pred[32,2,2]{2,1,0:T(4,128)(4,1)S(1)} %compare_and_fusion, bf16[32,2,1,2,128,128]{5,4,3,1,2,0:T(8,128)(2,1)} %bitcast.55), kind=kLoop, calls=%fused_computation.18 | loop fusion | flops 4194304 | bytes 16777344 | tf_op jit(solution)/shard_map/jit(_where)/select_n | solution.py:71
  109.6 97.9 %all_to_all.10 = bf16[32,2,1,2,128,128]{5,4,3,1,2,0:T(8,128)(2,1)} all-to-all(bf16[32,2,1,2,128,128]{5,4,3,1,2,0:T(8,128)(2,1)S(1)} %get-tuple-element.13), channel_id=1, replica_groups=mesh['row'=8,'col'=4] {'row','col'}, dimensions={0} | all-to-all | bytes 8388608 | tf_op jit(solution)/shard_map/all_to_all | solution.py:83
  207.5 3.8 all-to-all-start
  211.3 0.5 all-reduce.4.cloned.1.call-start
  212.2 19.9 %copy.46 = bf16[2,4096,896]{1,2,0:T(8,128)(2,1)} copy(bf16[2,4096,896]{2,1,0:T(8,128)(2,1)} %param.11) | data formatting | bytes 29360128 | tf_op args[2]
  232.6 4.2 gather_fusion.3
  236.9 4.5 copy.56
  241.4 7.4 %reshape.487 = bf16[2,896,896]{2,1,0:T(8,128)(2,1)} reshape(bf16[2,7,128,7,128]{4,3,2,1,0:T(8,128)(2,1)} %copy.56) | data formatting | bytes 6422528 | tf_op jit(solution)/shard_map/reshape | solution.py:102
  248.8 56.7 %all-to-all-done = bf16[32,2,1,2,128,128]{5,4,3,1,2,0:T(8,128)(2,1)} async-done(((bf16[32,2,1,2,128,128]{5,4,3,1,2,0:T(8,128)(2,1)}), bf16[32,2,1,2,128,128]{5,4,3,1,2,0:T(8,128)(2,1)}, u32[]{:S(2)}, u32[]{:S(2)}) %all-to-all-start) | async-done | bytes 4194336 | tf_op jit(solution)/shard_map/all_to_all | solution.py:82
  305.6 4.2 gather_fusion.1
  309.8 4.5 copy.51
  314.3 7.6 %reshape.485 = bf16[2,896,896]{2,1,0:T(8,128)(2,1)} reshape(bf16[2,7,128,7,128]{4,3,2,1,0:T(8,128)(2,1)} %copy.51) | data formatting | bytes 6422528 | tf_op jit(solution)/shard_map/reshape | solution.py:102
  321.9 23.4 %fusion.2 = f32[2,4096]{1,0:T(2,128)S(1)} fusion(bf16[2,896,896]{2,1,0:T(8,128)(2,1)S(1)} %copy-done, bf16[2,4096,896]{1,2,0:T(8,128)(2,1)} %copy.46, bf16[2,896]{1,0:T(2,128)(2,1)S(1)} %bitcast.68), kind=kOutput, calls=%fused_computation.9 | convolution fusion | flops 13190029312 | bytes 17927680 | tf_op jit(solution)/shard_map/bpi,bij->bpj/dot_general | solution.py:113
  345.3 24.4 %fusion.1 = f32[2,4096]{1,0:T(2,128)S(1)} fusion(bf16[2,896,896]{2,1,0:T(8,128)(2,1)} %reshape.485, bf16[2,4096,896]{1,2,0:T(8,128)(2,1)} %copy.46, bf16[2,896]{1,0:T(2,128)(2,1)S(1)} %bitcast.69), kind=kOutput, calls=%fused_computation.8 | convolution fusion | flops 13190029312 | bytes 17927680 | tf_op jit(solution)/shard_map/bpi,bij->bpj/dot_general | solution.py:113
  369.9 0.2 broadcast_multiply_fusion
  370.1 0.4 pad.4
  370.5 0.5 copy.69
  371.0 11.2 %fusion = f32[18,1024]{1,0:T(8,128)} fusion(f32[18,8192]{1,0:T(8,128)S(1)} %bitcast.64, s32[8192]{0:T(1024)S(1)} %bitcast.66), kind=kOutput, calls=%fused_computation.7 | convolution fusion | flops 1820327936 | bytes 696320 | tf_op jit(solution)/shard_map/dot_general | solution.py:123
  382.2 32.3 %all-reduce.4.cloned.1.call-done = f32[18,1024]{1,0:T(8,128)} async-done(((f32[18,1024]{1,0:T(8,128)}), f32[18,1024]{1,0:T(8,128)}) %all-reduce.4.cloned.1.call-update) | async-done | bytes 73744 | tf_op jit(solution)/shard_map/psum | solution.py:126
  414.5 1.6 reshape.449
  416.1 72.3 %all-reduce.6.cloned.1.call-done = f32[2,9,1024]{2,1,0:T(8,128)} async-done(((f32[2,9,1024]{2,1,0:T(8,128)}), f32[2,9,1024]{2,1,0:T(8,128)}) %all-reduce.6.cloned.1.call-update) | async-done | bytes 73744 | tf_op jit(solution)/shard_map/psum | solution.py:126
  488.3 1.6 copy.59
  (50 shorter events, 1.6 us)
Async XLA Ops:
  207.5 4.3 copy-start.5
  207.5 98.0 %all-to-all-start = ((bf16[32,2,1,2,128,128]{5,4,3,1,2,0:T(8,128)(2,1)}), bf16[32,2,1,2,128,128]{5,4,3,1,2,0:T(8,128)(2,1)}, u32[]{:S(2)}, u32[]{:S(2)}) async-start(bf16[32,2,1,2,128,128]{5,4,3,1,2,0:T(8,128)(2,1)} %get-tuple-element.12), calls=%async_computation | async-start | bytes 8388608 | tf_op jit(solution)/shard_map/all_to_all | solution.py:82
  211.3 203.1 %all-reduce.4.cloned.1.call-start = ((), (), s32[]{:S(2)}) async-start(), calls=%async_computation.2 | async-start | bytes 196608 | tf_op jit(solution)/shard_map/psum | solution.py:126
  212.1 20.0 %copy-start.7 = (s32[2]{0:T(128)S(1)}, s32[2]{0:T(128)}, u32[]{:S(2)}) copy-start(s32[2]{0:T(128)} %param.13) | copy-start | bytes 28
  212.1 20.1 %copy-start.4 = (s32[2,4096]{1,0:T(2,128)S(1)}, s32[2,4096]{1,0:T(2,128)}, u32[]{:S(2)}) copy-start(s32[2,4096]{1,0:T(2,128)} %param.17) | copy-start | bytes 98308
  212.1 20.1 %copy-start.1 = (f32[3,2,4096]{2,1,0:T(2,128)S(1)}, f32[3,2,4096]{2,1,0:T(2,128)}, u32[]{:S(2)}) copy-start(f32[3,2,4096]{2,1,0:T(2,128)} %param.15) | copy-start | bytes 294916
  212.1 20.3 %copy-start.3 = (f32[2,4096]{1,0:T(2,128)S(1)}, f32[2,4096]{1,0:T(2,128)}, u32[]{:S(2)}) copy-start(f32[2,4096]{1,0:T(2,128)} %param.16) | copy-start | bytes 98308
  314.3 7.6 %copy-start = (bf16[2,896,896]{2,1,0:T(8,128)(2,1)S(1)}, bf16[2,896,896]{2,1,0:T(8,128)(2,1)}, u32[]{:S(2)}) copy-start(bf16[2,896,896]{2,1,0:T(8,128)(2,1)} %reshape.487) | copy-start | bytes 9633796
  345.3 24.4 %copy-start.6 = (s32[2]{0:T(128)S(1)}, s32[2]{0:T(128)}, u32[]{:S(2)}) copy-start(s32[2]{0:T(128)} %param.14) | copy-start | bytes 28
  369.9 12.3 %copy-start.2 = (f32[2,2,4096]{2,1,0:T(2,128)}, f32[2,2,4096]{2,1,0:T(2,128)S(1)}, u32[]{:S(2)}) copy-start(f32[2,2,4096]{2,1,0:T(2,128)S(1)} %pad_maximum_fusion) | copy-start | bytes 196612
  382.2 106.2 %all-reduce.6.cloned.1.call-start = ((), (), s32[]{:S(2)}) async-start(), calls=%async_computation.3 | async-start | bytes 262144 | tf_op jit(solution)/shard_map/psum | solution.py:126
Sparse Core Ops, SparseCore 0:
  382.3 32.1 all-reduce.3
  417.8 70.4 all-reduce.5
